TPU v7x, 32 devices: a whole 2x2x4 slice. The times are simulated.
32 devices in a mesh: row: 8 (over z, y), col: 4 (over x, core).
Axes of the slice: x: 2, y: 2, z: 4, core: 2. Of those that a mesh axis runs over, the one named last changes fastest.
Arguments:
- densities: bfloat16 [4608, 3072], P(('row', 'col')), may hold values from -0.796875 to 0.796875
- counts: int32 [512], P(('row', 'col')), may hold values from 3 to 9
- coulomb: float32 [3072], replicated, may hold values from 0.05 to 1
- energies: float32 [4608], P(('row', 'col')), may hold values from 8 to 64
- vectors: bfloat16 [4608, 64], P(('row', 'col')), may hold values from -0.09375 to 0.09375
Outputs:
- kernel: float32 [4608, 4608], P('row', 'col')
- product: float32 [4608, 64], P(('row', 'col'))
All inputs are finite; a program needn't handle non-finite values.
Results may differ from a plain program's by a relative error of at most 0.0095.
Values may be sent and summed in bfloat16 or wider, within the bound.
A program may use at most 128 MiB of HBM per device.

v0:
```python
import functools

import jax
import jax.numpy as jnp
from jax import lax
from jax.experimental import pallas as pl
from jax.experimental.pallas import tpu as pltpu
from jax.sharding import PartitionSpec as P

SLOT = 9
MESH = pl.DeviceIdType.MESH
NT = (((1,), (1,)), ((), ()))
NN = (((1,), (0,)), ((), ()))


def pack(v):
    lanes = 128
    rest = v.shape[1] % lanes
    height = v.shape[0] * rest // lanes
    tail = jnp.concatenate(
        [v[j * height:(j + 1) * height, lanes:] for j in range(lanes // rest)], axis=1)
    return jnp.concatenate([v[:, :lanes], tail], axis=0)


def unpack(p, nv, rest):
    lanes = 128
    tail = jnp.concatenate(
        [p[nv:, j * rest:(j + 1) * rest] for j in range(lanes // rest)], axis=0)
    return jnp.concatenate([p[:nv], tail], axis=1)


def exchange_kernel(n_row, n_col, raw_ref, counts_ref, energies_ref, vt_ref, coulomb_ref, out_ref, prod_ref,
                    own_ref, part_ref, d_ref, v_ref, cols, rows_raw, weighted, vecs, psend, q, qsend, qrecv, qpiece, qland,
                    local_sem, y_send, y_recv, up_send, down_send, z_recv, x_send, x_recv,
                    core_send, core_recv, v_send, v_recv, p_send, p_recv, q_send, q_recv, c_send, c_recv):
    line, chips = n_row // 2, n_col // 2
    r, c = lax.axis_index("row"), lax.axis_index("col")
    z, y = r // 2, lax.rem(r, 2)
    x, core = c // 2, lax.rem(c, 2)
    other_y, other_core = 1 - y, 1 - core
    block = d_ref.shape[1]
    half = d_ref.shape[2]
    nv = prod_ref.shape[0]

    barrier = pltpu.get_barrier_semaphore()
    for step in range(1, n_row):
        pl.semaphore_signal(barrier, inc=1, device_id=(lax.rem(r + step, n_row), c), device_id_type=MESH)
    for step in range(1, n_col):
        pl.semaphore_signal(barrier, inc=1, device_id=(r, lax.rem(c + step, n_col)), device_id_type=MESH)

    kpoints = counts_ref.shape[1]
    counts = counts_ref[...].astype(jnp.float32)
    row_index = lax.broadcasted_iota(jnp.int32, (block, kpoints), 0)
    kpoint = lax.broadcasted_iota(jnp.int32, (block, kpoints), 1)
    slot = row_index - SLOT * kpoint
    inside = (slot >= 0) & (slot < SLOT) & (slot.astype(jnp.float32) < counts)
    usable = jnp.sum(jnp.where(inside, 1.0, 0.0), axis=1, keepdims=True)
    for part in range(2):
        piece = raw_ref[:, part * half:(part + 1) * half].astype(jnp.float32)
        d_ref[part] = jnp.where(usable > 0.5, piece, 0.0).astype(jnp.bfloat16)
    vt = vt_ref[...].astype(jnp.float32)
    v_ref[...] = pack(vt).astype(jnp.bfloat16)
    pl.semaphore_wait(barrier, n_row + n_col - 2)

    partner = (z * 2 + other_y, c)
    sibling = (r, x * 2 + other_core)

    def remote(src, dst, send, recv, device):
        return pltpu.make_async_remote_copy(
            src_ref=src, dst_ref=dst, send_sem=send, recv_sem=recv, device_id=device, device_id_type=MESH)

    def y_copy():
        return remote(d_ref.at[other_y], cols.at[z, y], y_send, y_recv, partner)

    def y_arrival():
        return remote(d_ref.at[other_y], cols.at[z, other_y], y_send, y_recv, partner)

    def up(src, zp, s):
        return remote(src, cols.at[zp, s], up_send.at[zp, s], z_recv.at[zp, s], ((z + 1) * 2 + y, c))

    def down(src, zp, s):
        return remote(src, cols.at[zp, s], down_send.at[zp, s], z_recv.at[zp, s], ((z - 1) * 2 + y, c))

    def x_copy(src, s, step):
        return remote(src, rows_raw.at[s, c], x_send.at[s, step], x_recv.at[s, x],
                      (r, lax.rem(x + step, chips) * 2 + core))

    def x_arrival(s, step):
        xs = lax.rem(x + chips - step, chips)
        return remote(d_ref.at[0], rows_raw.at[s, xs * 2 + core], x_send.at[s, step], x_recv.at[s, xs], sibling)

    def core_copy(src, s, xs):
        return remote(src, rows_raw.at[s, xs * 2 + core], core_send.at[s, xs], core_recv.at[s, xs], sibling)

    def core_arrival(s, xs):
        return remote(d_ref.at[0], rows_raw.at[s, xs * 2 + other_core], core_send.at[s, xs], core_recv.at[s, xs],
                      sibling)

    def spread(src, s):
        @pl.when(z < line - 1)
        def _():
            up(src, z, s).start()

        @pl.when(z > 0)
        def _():
            down(src, z, s).start()

        for step in range(1, chips):
            x_copy(src, s, step).start()
        core_copy(src, s, x).start()

    def relay(zp, s):
        @pl.when((zp < z) & (z < line - 1))
        def _():
            up(cols.at[zp, s], zp, s).start()

        @pl.when((zp > z) & (z > 0))
        def _():
            down(cols.at[zp, s], zp, s).start()

    def z_wait(zp, s):
        remote(cols.at[zp, s], cols.at[zp, s], up_send.at[zp, s], z_recv.at[zp, s], sibling).wait_recv()

    y_copy().start()
    spread(d_ref.at[y], y)
    for step in range(1, n_row):
        remote(v_ref, vecs.at[r], v_send.at[step], v_recv.at[r], (lax.rem(r + step, n_row), c)).start()
    locals_ = [
        pltpu.make_async_copy(d_ref.at[y], cols.at[z, y], local_sem.at[0]),
        pltpu.make_async_copy(d_ref.at[y], rows_raw.at[y, c], local_sem.at[1]),
        pltpu.make_async_copy(v_ref, vecs.at[r], local_sem.at[2]),
    ]
    for copy in locals_:
        copy.start()
    q[...] = jnp.zeros_like(q)
    for copy in locals_:
        copy.wait()

    y_arrival().wait_recv()
    spread(cols.at[z, other_y], other_y)
    late = pltpu.make_async_copy(cols.at[z, other_y], rows_raw.at[other_y, c], local_sem.at[3])
    late.start()

    def share(s):
        for step in range(1, chips):
            xs = lax.rem(x + chips - step, chips)
            x_arrival(s, step).wait_recv()
            core_copy(rows_raw.at[s, xs * 2 + core], s, xs).start()

    def weigh(s):
        for xs in range(chips):
            core_arrival(s, xs).wait_recv()
        for cp in range(n_col):
            weighted[s, cp * block:(cp + 1) * block, :] = (
                rows_raw[s, cp].astype(jnp.float32) * coulomb_ref[y]).astype(jnp.bfloat16)

    def neighbours(s):
        for zp in (z - 1, z + 1):
            @pl.when((zp >= 0) & (zp < line))
            def _():
                z_wait(zp, s)
                relay(zp, s)

    share(y)
    neighbours(y)
    weigh(y)
    late.wait()
    share(other_y)
    neighbours(other_y)
    weigh(other_y)
    for step in range(1, n_row):
        rp = lax.rem(r + step, n_row)
        remote(v_ref, vecs.at[rp], v_send.at[step], v_recv.at[rp], partner).wait_recv()

    def p_copy(rp):
        return remote(psend.at[rp], part_ref.at[rp], p_send.at[rp], p_recv.at[rp], partner)

    def vector(rp):
        return unpack(vecs[rp].astype(jnp.float32), nv, block % 128).astype(jnp.bfloat16)

    def pair(t, carry):
        zp = z + jnp.where(t == 0, 0, 2 * t - 3)

        @pl.when((zp >= 0) & (zp < line))
        def _():
            both = cols[zp].reshape(2 * block, half)
            away = lax.dot_general(both, weighted[other_y], NT,
                                   preferred_element_type=jnp.float32).astype(jnp.bfloat16)
            for s in range(2):
                tile = away[s * block:(s + 1) * block]
                psend[zp * 2 + s] = tile
                q[1] += lax.dot_general(vector(zp * 2 + s), tile, NN, preferred_element_type=jnp.float32)
            for s in range(2):
                p_copy(zp * 2 + s).start()
            home = lax.dot_general(both, weighted[y], NT, preferred_element_type=jnp.float32)
            for s in range(2):
                tile = home[s * block:(s + 1) * block]
                own_ref[zp * 2 + s] = tile
                q[0] += lax.dot_general(vector(zp * 2 + s), tile.astype(jnp.bfloat16), NN,
                                        preferred_element_type=jnp.float32)
        return carry

    lax.fori_loop(0, 3, pair, 0)

    q_copy = remote(qsend, qrecv, q_send, q_recv, partner)
    slots = 4 * (line - 2)
    last = 4 * (jnp.maximum(z, line - 1 - z) - 2) + 2 + jnp.where(z < line - 1 - z, 1, 0)

    def finish(d, k):
        side = 2 * lax.rem(k, 2) - 1
        zp = z + d * side
        s = jnp.where(k < 2, other_y, y)

        @pl.when((zp >= 0) & (zp < line) & ((d > 0) | (side > 0)))
        def _():
            rp = zp * 2 + s
            p_copy(rp).wait_recv()
            tile = (own_ref[rp] + part_ref[rp].astype(jnp.float32)).T.astype(jnp.bfloat16)
            for block_index in range(n_row):
                @pl.when(rp == block_index)
                def _():
                    out_ref[:, block_index * block:(block_index + 1) * block] = tile

    def finish_all(d):
        def step(k, carry):
            finish(d, k)
            return carry

        lax.fori_loop(0, 4, step, 0)

    def single(t, carry):
        d = t // 4 + 2
        s = jnp.where(lax.rem(t // 2, 2) == 0, y, other_y)
        zp = z + d * (2 * lax.rem(t, 2) - 1)

        @pl.when((zp >= 0) & (zp < line))
        def _():
            z_wait(zp, s)
            relay(zp, s)
            rp = zp * 2 + s
            v = vector(rp)
            away = lax.dot_general(cols[zp, s], weighted[other_y], NT,
                                   preferred_element_type=jnp.float32).astype(jnp.bfloat16)
            psend[rp] = away
            q[1] += lax.dot_general(v, away, NN, preferred_element_type=jnp.float32)

            @pl.when(t == last)
            def _():
                qsend[...] = q[1].astype(jnp.bfloat16)
                q_copy.start()

            p_copy(rp).start()
            home = lax.dot_general(cols[zp, s], weighted[y], NT, preferred_element_type=jnp.float32)
            own_ref[rp] = home
            q[0] += lax.dot_general(v, home.astype(jnp.bfloat16), NN, preferred_element_type=jnp.float32)

        @pl.when(lax.rem(t, 4) == 1)
        def _():
            finish_all(d - 2)

        @pl.when(t == slots - 3)
        def _():
            finish_all(line - 2)
        return carry

    lax.fori_loop(0, slots, single, 0)
    q_copy.wait()
    total = q[0] + qrecv[...].astype(jnp.float32)
    for cp in range(n_col):
        qpiece[cp] = total[:, cp * block:(cp + 1) * block].astype(jnp.bfloat16)

    def c_copy(step):
        to = lax.rem(c + step, n_col)
        return remote(qpiece.at[to], qland.at[c], c_send.at[step], c_recv.at[c], (r, to))

    for step in range(1, n_col):
        c_copy(step).start()
    answer = qpiece[c].astype(jnp.float32)
    for step in range(1, n_col):
        source = lax.rem(c + step, n_col)
        remote(qpiece.at[0], qland.at[source], c_send.at[step], c_recv.at[source], sibling).wait_recv()
        answer += qland[source].astype(jnp.float32)
    lane_slot = (lax.broadcasted_iota(jnp.int32, (kpoints, block), 1)
                 - SLOT * lax.broadcasted_iota(jnp.int32, (kpoints, block), 0))
    mine = jnp.where((lane_slot >= 0) & (lane_slot < SLOT), 1.0, 0.0)
    limit = lax.dot_general(jnp.broadcast_to(counts, (8, kpoints)), mine, NN, preferred_element_type=jnp.float32)[:1]
    lane_slot = lax.rem(lax.broadcasted_iota(jnp.int32, (1, block), 1), SLOT).astype(jnp.float32)
    diagonal = jnp.where(lane_slot + 0.5 < limit, energies_ref[...], 0.0)
    prod_ref[...] = answer + diagonal * vt_ref[...].astype(jnp.float32)

    finish_all(line - 1)
    y_copy().wait_send()
    for step in range(1, n_col):
        c_copy(step).wait_send()
    for step in range(1, n_row):
        remote(v_ref, vecs.at[r], v_send.at[step], v_recv.at[r], partner).wait_send()
    for s in range(2):
        for step in range(1, chips):
            x_copy(d_ref.at[0], s, step).wait_send()
        for xs in range(chips):
            core_copy(d_ref.at[0], s, xs).wait_send()
        for zp in range(line):
            @pl.when((zp <= z) & (z < line - 1))
            def _():
                up(d_ref.at[0], zp, s).wait_send()

            @pl.when((zp >= z) & (z > 0))
            def _():
                down(d_ref.at[0], zp, s).wait_send()
    for rp in range(n_row):
        p_copy(rp).wait_send()


def body(n_row, n_col, densities, counts, coulomb, energies, vectors):
    rows, depth = densities.shape
    nv = vectors.shape[1]
    half = depth // 2
    line, chips = n_row // 2, n_col // 2
    bf16, f32 = jnp.bfloat16, jnp.float32
    packed = jax.eval_shape(pack, jax.ShapeDtypeStruct((nv, rows), bf16))
    vmem = pl.BlockSpec(memory_space=pltpu.VMEM)
    dma = pltpu.SemaphoreType.DMA
    wide = n_col * rows
    kernel, prod = pl.pallas_call(
        functools.partial(exchange_kernel, n_row, n_col),
        out_shape=(
            jax.ShapeDtypeStruct((wide, n_row * rows), bf16),
            jax.ShapeDtypeStruct((nv, rows), f32),
        ),
        in_specs=[vmem] * 5,
        out_specs=(vmem, vmem),
        scratch_shapes=[
            pltpu.VMEM((n_row, rows, wide), f32),
            pltpu.VMEM((n_row, rows, wide), bf16),
            pltpu.VMEM((2, rows, half), bf16),
            pltpu.VMEM(packed.shape, bf16),
            pltpu.VMEM((line, 2, rows, half), bf16),
            pltpu.VMEM((2, n_col, rows, half), bf16),
            pltpu.VMEM((2, wide, half), bf16),
            pltpu.VMEM((n_row,) + packed.shape, bf16),
            pltpu.VMEM((n_row, rows, wide), bf16),
            pltpu.VMEM((2, nv, wide), f32),
            pltpu.VMEM((nv, wide), bf16),
            pltpu.VMEM((nv, wide), bf16),
            pltpu.VMEM((n_col, nv, rows), bf16),
            pltpu.VMEM((n_col, nv, rows), bf16),
            dma((4,)), dma, dma, dma((line, 2)), dma((line, 2)), dma((line, 2)),
            dma((2, chips)), dma((2, chips)), dma((2, chips)), dma((2, chips)),
            dma((n_row,)), dma((n_row,)), dma((n_row,)), dma((n_row,)), dma, dma,
            dma((n_col,)), dma((n_col,)),
        ],
        compiler_params=pltpu.CompilerParams(
            collective_id=0, has_side_effects=True, vmem_limit_bytes=60 * 2**20),
    )(densities, counts[None], energies[None], vectors.T, coulomb.reshape(2, 1, half))
    return (kernel.astype(f32), prod.T)


def solution(mesh):
    return jax.shard_map(
        functools.partial(body, mesh.shape["row"], mesh.shape["col"]),
        mesh=mesh,
        in_specs=(
            P(("row", "col"), None),
            P(("row", "col")),
            P(),
            P(("row", "col")),
            P(("row", "col"), None),
        ),
        out_specs=(P("row", "col"), P(("row", "col"), None)),
        check_vma=False,
    )
```

profile of v0, /device:TPU:0, one launch (start us, length us, event | category | flops | bytes accessed | tf_op | source)
XLA Modules:
  0.0 83.0 jit_solution(3359359552664236300)
XLA Ops:
  0.6 78.6 %shard_map.68 = (bf16[576,1152]{1,0:T(8,128)(2,1)}, f32[64,144]{1,0:T(8,128)}) custom-call(bf16[144,3072]{1,0:T(8,128)(2,1)} %raw_ref.1, s32[1,16]{1,0:T(1,128)} %bitcast.9, f32[1,144]{1,0:T(1,128)} %bitcast.8, bf16[64,144]{1,0:T(8,128)(2,1)} %bitcast.6, f32[2,1,1536]{2,1,0:T(1,128)} %bitcast.7), custom_call_target="tpu_custom_call" | custom-call | tf_op jit(solution)/shard_map/pallas_call | solution.py:324
  79.3 0.0 copy-start
  79.3 3.0 %convert_element_type.3 = f32[576,1152]{1,0:T(8,128)} convert(bf16[576,1152]{1,0:T(8,128)(2,1)} %get-tuple-element.4) | non-fusion elementwise | flops 663552 | bytes 3981312 | tf_op jit(solution)/shard_map/convert_element_type | solution.py:355
  82.3 0.0 copy-done
  82.3 0.6 copy.8
Async XLA Ops:
  79.3 3.1 %copy-start = (f32[64,144]{1,0:T(8,128)S(1)}, f32[64,144]{1,0:T(8,128)}, u32[]{:S(2)}) copy-start(f32[64,144]{1,0:T(8,128)} %get-tuple-element.5) | copy-start | bytes 110596
where the time goes:
time: 83.1 us; the launch traced here: 83 us
  Pallas kernels  78.6 us (95%)
  other arithmetic  3.04 us (4%)
    pallas_call x1, Pallas kernels, body(): pl.pallas_call(functools.partial(exchange_kernel, n_row, n_col), out_shap...  78.6 us
    convert_element_type x1, other arithmetic, body(): return (kernel.astype(f32), prod.T)  3.04 us

commit v1 on v0

v1 whole, which is shorter than its diff:
```python
import functools

import jax
import jax.numpy as jnp
from jax import lax
from jax.experimental import pallas as pl
from jax.experimental.pallas import tpu as pltpu
from jax.sharding import PartitionSpec as P

SLOT = 9
LANES = 128
MESH = pl.DeviceIdType.MESH
NT = (((1,), (1,)), ((), ()))
NN = (((1,), (0,)), ((), ()))


def pack(v, groups):
    height = v.shape[0] // groups
    tail = jnp.concatenate([v[j * height:(j + 1) * height, LANES:] for j in range(groups)], axis=1)
    spare = LANES - tail.shape[1]
    if spare:
        tail = jnp.concatenate([tail, jnp.zeros((height, spare), v.dtype)], axis=1)
    return jnp.concatenate([v[:, :LANES], tail], axis=0)


def unpack(p, rows, rest, groups):
    tail = jnp.concatenate([p[rows:, j * rest:(j + 1) * rest] for j in range(groups)], axis=0)
    return jnp.concatenate([p[:rows], tail], axis=1)


def groups_of(rows, rest):
    return max(g for g in range(1, LANES // rest + 1) if rows % g == 0 and rows // g % 8 == 0)


def plan(line):
    pairs = [(i, j) for i in range(line) for j in range(i + 1, line)]
    modes = {6: "jjbiii"}.get(len(pairs), "b" * len(pairs))
    computed = [[i] for i in range(line)]
    exports = [[] for _ in range(line)]
    high, low = list(range(line)), list(range(line))
    for (i, j), mode in zip(pairs, modes):
        if mode in "jb":
            computed[j].append(i)
            high[i] = max(high[i], j)
        if mode in "ib":
            computed[i].append(j)
            low[j] = min(low[j], i)
        if mode == "j":
            exports[j].append(i)
        if mode == "i":
            exports[i].append(j)
    special = len(pairs) == 6
    held = [special and low[i] < i and any(low[j] < i for j in range(i + 1, line)) for i in range(line)]
    if special:
        order = [[None, None, 3], [0, 3, 2], [3, 0, None], [None, None, 0]]
    else:
        order = [sorted((j for j in range(line) if j != i), key=lambda j: abs(i - j)) for i in range(line)]
    return computed, exports, high, low, held, order


def look(index, values):
    out = jnp.int32(0)
    for i, value in enumerate(values):
        out = jnp.where(index == i, jnp.int32(value), out)
    return out


def among(a, b, table):
    out = jnp.bool_(False)
    for i, row in enumerate(table):
        for j in row:
            out = out | ((a == i) & (b == j))
    return out


def exchange_kernel(n_row, n_col, chunks, raw_ref, counts_ref, energies_ref, vt_ref, coulomb_ref, out_ref, prod_ref,
                    rows, cols, buf, ysend, tsend, tland, vline, vland, vplane, q, back, bsend, bland, qsend, qland,
                    up_send, down_send, z_recv, xs_send, xf_send, ys_send, yf_send, sib_send, r_recv, s_recv,
                    vp_send, vp_recv, vl_send, vl_recv, yr_send, yr_recv, t_send, t_recv, b_send, b_recv,
                    q_send, q_recv):
    line, chips = n_row // 2, n_col // 2
    computed, exports, high, low, held, order = plan(line)
    special = any(exports)
    r, c = lax.axis_index("row"), lax.axis_index("col")
    z, y = r // 2, lax.rem(r, 2)
    x, core = c // 2, lax.rem(c, 2)
    other_y, other_core = 1 - y, 1 - core
    block, depth = raw_ref.shape
    half = depth // 2
    chunk = block // chunks
    nv = prod_ref.shape[0]
    rest = block % LANES
    vgroups, tgroups = groups_of(nv, rest), groups_of(block, rest)
    place = y * n_col + c
    plane = 2 * n_col
    f32, bf16 = jnp.float32, jnp.bfloat16

    barrier = pltpu.get_barrier_semaphore()
    for step in range(1, plane):
        t = lax.rem(place + step, plane)
        pl.semaphore_signal(barrier, inc=1, device_id=(z * 2 + t // n_col, lax.rem(t, n_col)), device_id_type=MESH)
    for step in range(1, line):
        for cc in range(n_col):
            pl.semaphore_signal(barrier, inc=1, device_id=(lax.rem(z + step, line) * 2 + y, cc), device_id_type=MESH)

    kpoints = counts_ref.shape[1]
    counts = counts_ref[...].astype(f32)
    row_index = lax.broadcasted_iota(jnp.int32, (block, kpoints), 0)
    kpoint = lax.broadcasted_iota(jnp.int32, (block, kpoints), 1)
    slot = row_index - SLOT * kpoint
    inside = (slot >= 0) & (slot < SLOT) & (slot.astype(f32) < counts)
    usable = jnp.sum(jnp.where(inside, 1.0, 0.0), axis=1, keepdims=True)
    d = jnp.where(usable > 0.5, raw_ref[...].astype(f32), 0.0)
    rows[y, c] = d.astype(bf16)
    cols[z] = (d * coulomb_ref[...]).astype(bf16)
    v_mine = pack(vt_ref[...].astype(f32), vgroups).astype(bf16)
    vline[z] = v_mine
    vland[y, c] = v_mine
    pl.semaphore_wait(barrier, plane - 1 + (line - 1) * n_col)

    partner = (z * 2 + other_y, c)
    sibling = (r, x * 2 + other_core)

    def remote(src, dst, send, recv, device):
        return pltpu.make_async_remote_copy(
            src_ref=src, dst_ref=dst, send_sem=send, recv_sem=recv, device_id=device, device_id_type=MESH)

    def piece(zp, ch):
        return cols.at[zp, pl.ds(ch * chunk, chunk)]

    def up(zp, ch):
        return remote(piece(zp, ch), piece(zp, ch), up_send.at[zp, ch], z_recv.at[zp, ch], ((z + 1) * 2 + y, c))

    def down(zp, ch):
        return remote(piece(zp, ch), piece(zp, ch), down_send.at[zp, ch], z_recv.at[zp, ch], ((z - 1) * 2 + y, c))

    def part(yy, cc, h):
        return rows.at[yy, cc, :, pl.ds(h * half, half)]

    def x_peer(step):
        return (r, lax.rem(x + step, chips) * 2 + core)

    def x_own(step, h):
        return remote(part(y, c, h), part(y, c, h), xs_send.at[step, h], r_recv.at[y, x, h], x_peer(step))

    def x_forward(step):
        return remote(part(other_y, c, 1), part(other_y, c, 1), xf_send.at[step], r_recv.at[other_y, x, 1], x_peer(step))

    def y_own(h):
        return remote(part(y, c, h), part(y, c, h), ys_send.at[h], r_recv.at[y, x, h], partner)

    def y_forward(xx):
        cc = xx * 2 + core
        return remote(part(y, cc, 0), part(y, cc, 0), yf_send.at[xx], r_recv.at[y, xx, 0], partner)

    def share(yy, xx, h):
        cc = xx * 2 + core
        return remote(part(yy, cc, h), part(yy, cc, h), sib_send.at[yy, xx, h], s_recv.at[yy, xx, h], sibling)

    def arrive(yy, xx, h):
        cc = xx * 2 + core
        remote(part(yy, cc, h), part(yy, cc, h), sib_send.at[yy, xx, h], r_recv.at[yy, xx, h], sibling).wait_recv()
        share(yy, xx, h).start()

    def shared(yy):
        for xx in range(chips):
            for h in range(2):
                cc = xx * 2 + other_core
                remote(part(yy, cc, h), part(yy, cc, h), sib_send.at[yy, xx, h], s_recv.at[yy, xx, h],
                       sibling).wait_recv()

    goes_up = look(z, [high[i] > i for i in range(line)]) > 0
    goes_down = look(z, [low[i] < i for i in range(line)]) > 0
    holds = look(z, held) > 0

    for ch in range(chunks):
        @pl.when(goes_up)
        def _():
            up(z, ch).start()

        @pl.when(goes_down & (~holds if ch else goes_down))
        def _():
            down(z, ch).start()
    for h in range(2):
        share(y, x, h).start()
        for step in range(1, chips):
            x_own(step, h).start()
        y_own(h).start()

    def v_plane(step):
        t = lax.rem(place + step, plane)
        return remote(vline.at[z], vland.at[y, c], vp_send.at[step], vp_recv.at[place],
                      (z * 2 + t // n_col, lax.rem(t, n_col)))

    def v_line(zt):
        return remote(vline.at[z], vline.at[z], vl_send.at[zt], vl_recv.at[z], (zt * 2 + y, c))

    for step in range(1, plane):
        v_plane(step).start()
    for zt in range(line):
        @pl.when((z != zt) & among(zt, z, computed))
        def _():
            v_line(zt).start()
    q[...] = jnp.zeros_like(q)

    def z_event(h, ch, late=False):
        if not late:
            below = z - h

            @pl.when((below >= 0) & (look(below, high) >= z))
            def _():
                remote(piece(below, ch), piece(below, ch), up_send.at[below, ch], z_recv.at[below, ch],
                       sibling).wait_recv()

                @pl.when(look(below, high) > z)
                def _():
                    up(below, ch).start()
        above = z + h
        mine = (above < line) & (look(above, low) <= z)
        if ch:
            mine = mine & ((look(above, held) > 0) == late)

        @pl.when(mine)
        def _():
            remote(piece(above, ch), piece(above, ch), down_send.at[above, ch], z_recv.at[above, ch],
                   sibling).wait_recv()

            @pl.when(look(above, low) < z)
            def _():
                down(above, ch).start()
        if h == 1 and ch == chunks - 1 and not late:
            for later in range(1, chunks):
                @pl.when(holds)
                def _():
                    down(z, later).start()

    def x_event(h):
        for step in range(1, chips):
            xs = lax.rem(x + chips - step, chips)
            arrive(y, xs, h)
            if h == 0:
                y_forward(xs).start()

    def y_event(h):
        arrive(other_y, x, h)
        if h == 1:
            for step in range(1, chips):
                x_forward(step).start()

    def far_event(h):
        for step in range(1, chips):
            arrive(other_y, lax.rem(x + chips - step, chips), h)

    def y_result(zi):
        return remote(ysend.at[zi], buf.at[zi, y], yr_send.at[zi], yr_recv.at[zi], partner)

    def tile_copy(zi, yy, cc):
        return remote(tsend.at[zi, yy, cc], tland.at[z, yy, c], t_send.at[zi, yy, cc], t_recv.at[z, yy, c],
                      (zi * 2 + y, cc))

    def back_copy(zi):
        return remote(bsend.at[zi], bland.at[z], b_send.at[zi], b_recv.at[z], (zi * 2 + y, c))

    def multiply(zi, near):
        yy = y if near else other_y
        both = rows[yy].reshape(n_col * block, depth)
        tile = lax.dot_general(cols[zi], both, NT, preferred_element_type=f32)
        small = tile.astype(bf16)
        if near:
            own = zi == line
            buf[jnp.where(own, z, zi), jnp.where(own, other_y, y)] = small
        else:
            ysend[zi] = small
            y_result(zi).start()
        if special:
            @pl.when(among(z, zi, exports))
            def _():
                for cc in range(n_col):
                    tsend[zi, yy, cc] = pack(tile[:, cc * block:(cc + 1) * block], tgroups).astype(bf16)
                for cc in range(n_col):
                    tile_copy(zi, yy, cc).start()
                term = lax.dot_general(vplane[yy], small, NT, preferred_element_type=f32)
                if near:
                    back[zi] = term
                else:
                    bsend[zi] = pack(back[zi] + term, vgroups).astype(bf16)
                    back_copy(zi).start()
        v = unpack(vline[zi].astype(f32), nv, rest, vgroups).astype(bf16)
        q[yy] += lax.dot_general(v, small, NN, preferred_element_type=f32)

    def v_wait(zi):
        remote(vline.at[zi], vline.at[zi], vl_send.at[zi], vl_recv.at[zi], sibling).wait_recv()

    ranks = len(order[0])
    rank_of = [[-1 if row[k] is None else row[k] for row in order] for k in range(ranks)]

    def ranked(k, near):
        zi = look(z, rank_of[k])

        @pl.when(zi >= 0)
        def _():
            if near:
                v_wait(zi)
            multiply(zi, near)

    def first(with_rank):
        for yy in range(2):
            for cc in range(n_col):
                source = yy * n_col + cc

                @pl.when(place != source)
                def _():
                    remote(vline.at[0], vland.at[yy, cc], vp_send.at[0], vp_recv.at[source], sibling).wait_recv()
        vline[line] = vland[other_y, c]
        for yy in range(2):
            vplane[yy] = jnp.concatenate(
                [unpack(vland[yy, cc].astype(f32), nv, rest, vgroups) for cc in range(n_col)], axis=1).astype(bf16)
        cols[line] = (rows[other_y, c].astype(f32) * coulomb_ref[...]).astype(bf16)
        extra = look(z, rank_of[0]) if with_rank else jnp.int32(-1)

        def body(t, carry):
            zi = jnp.where(t == 0, z, jnp.where(t == 1, line, extra))

            @pl.when(zi >= 0)
            def _():
                @pl.when(t == 2)
                def _():
                    v_wait(zi)
                multiply(zi, True)
            return carry

        lax.fori_loop(0, 3 if with_rank else 2, body, 0)

    def place_computed(zz):
        @pl.when(among(z, jnp.int32(zz), computed))
        def _():
            @pl.when(z != zz)
            def _():
                remote(ysend.at[zz], buf.at[zz, other_y], yr_send.at[zz], yr_recv.at[zz], partner).wait_recv()
            out_ref[:, 2 * zz * block:2 * (zz + 1) * block] = (
                buf[zz].reshape(2 * block, n_col * block).astype(f32).T.astype(bf16))

    def place_imported(zz):
        @pl.when(among(jnp.int32(zz), z, exports))
        def _():
            for cc in range(n_col):
                tiles = []
                for yy in range(2):
                    remote(tsend.at[0, 0, 0], tland.at[zz, yy, cc], t_send.at[zz, yy, cc], t_recv.at[zz, yy, cc],
                           partner).wait_recv()
                    tiles.append(unpack(tland[zz, yy, cc].astype(f32), block, rest, tgroups))
                out_ref[cc * block:(cc + 1) * block, 2 * zz * block:2 * (zz + 1) * block] = (
                    jnp.concatenate(tiles, axis=1).astype(bf16))

    events = [(h + ch + 0.24 * h, functools.partial(z_event, h, ch)) for h in range(1, line) for ch in range(chunks)]
    wide = chunks / 2
    events += [
        (wide + 0.25, functools.partial(x_event, 0)), (wide + 0.26, functools.partial(y_event, 0)),
        (2 * wide + 0.25, functools.partial(x_event, 1)), (2 * wide + 0.26, functools.partial(y_event, 1)),
        (3 * wide + 0.25, functools.partial(far_event, 0)), (3 * wide + 0.5, functools.partial(far_event, 1)),
    ]
    if special:
        second = 1 + chunks + 0.48
        events += [
            (second - 0.02, lambda: (shared_near(), first(True))),
            (second + 0.01, lambda: ranked(1, True)),
            (3 * wide + 0.51, lambda: shared(other_y)),
            (3 * wide + 0.52, lambda: lax.fori_loop(0, 2, far_pair, 0)),
            (3 * wide + 0.53, lambda: place_self()),
        ]

    def shared_near():
        shared(y)

    def far_pair(t, carry):
        zi = jnp.where(t == 0, look(z, rank_of[0]), look(z, rank_of[1]))

        @pl.when(zi >= 0)
        def _():
            multiply(zi, False)
        return carry

    def place_self():
        for zz in range(line):
            @pl.when(z == zz)
            def _():
                out_ref[:, 2 * zz * block:2 * (zz + 1) * block] = (
                    buf[zz].reshape(2 * block, n_col * block).astype(f32).T.astype(bf16))

    for _, event in sorted(events, key=lambda e: e[0]):
        event()
    if special:
        for ch in range(1, chunks):
            z_event(1, ch, True)
        ranked(2, True)
        ranked(2, False)
    else:
        shared(y)
        shared(other_y)
        first(False)
        place_self()

        def every(t, carry):
            zi = lax.rem(z + 1 + t, line)
            v_wait(zi)
            multiply(zi, True)
            multiply(zi, False)
            return carry

        lax.fori_loop(0, line - 1, every, 0)

    for yy in range(2):
        for cc in range(n_col):
            qsend[yy * n_col + cc] = pack(q[yy][:, cc * block:(cc + 1) * block], vgroups).astype(bf16)

    def q_copy(step):
        t = lax.rem(place + step, plane)
        return remote(qsend.at[t], qland.at[place], q_send.at[step], q_recv.at[place],
                      (z * 2 + t // n_col, lax.rem(t, n_col)))

    for step in range(1, plane):
        q_copy(step).start()

    for zz in range(line):
        @pl.when(z != zz)
        def _():
            place_computed(zz)

    answer = qsend[place].astype(f32)
    for step in range(1, plane):
        source = lax.rem(place + step, plane)
        remote(qsend.at[0], qland.at[source], q_send.at[step], q_recv.at[source], sibling).wait_recv()
        answer += qland[source].astype(f32)
    back[line] = unpack(answer, nv, rest, vgroups)
    for zz in range(line):
        @pl.when(among(jnp.int32(zz), z, exports))
        def _():
            remote(bsend.at[0], bland.at[zz], b_send.at[0], b_recv.at[zz], sibling).wait_recv()
            back[line] += unpack(bland[zz].astype(f32), nv, rest, vgroups)
    lane_slot = (lax.broadcasted_iota(jnp.int32, (kpoints, block), 1)
                 - SLOT * lax.broadcasted_iota(jnp.int32, (kpoints, block), 0))
    mine = jnp.where((lane_slot >= 0) & (lane_slot < SLOT), 1.0, 0.0)
    limit = lax.dot_general(jnp.broadcast_to(counts, (8, kpoints)), mine, NN, preferred_element_type=f32)[:1]
    lane_slot = lax.rem(lax.broadcasted_iota(jnp.int32, (1, block), 1), SLOT).astype(f32)
    diagonal = jnp.where(lane_slot + 0.5 < limit, energies_ref[...], 0.0)
    prod_ref[...] = back[line] + diagonal * vt_ref[...].astype(f32)

    if special:
        for zz in range(line):
            place_imported(zz)

    for ch in range(chunks):
        for zp in range(line):
            @pl.when((zp <= z) & (high[zp] > z))
            def _():
                up(zp, ch).wait_send()

            @pl.when((zp >= z) & (low[zp] < z))
            def _():
                down(zp, ch).wait_send()
    for h in range(2):
        y_own(h).wait_send()
        for step in range(1, chips):
            x_own(step, h).wait_send()
        for yy in range(2):
            for xx in range(chips):
                share(yy, xx, h).wait_send()
    for step in range(1, chips):
        x_forward(step).wait_send()
        y_forward(lax.rem(x + step, chips)).wait_send()
    for step in range(1, plane):
        v_plane(step).wait_send()
        q_copy(step).wait_send()
    for zz in range(line):
        @pl.when((z != zz) & among(jnp.int32(zz), z, computed))
        def _():
            v_line(zz).wait_send()

        @pl.when((z != zz) & among(z, jnp.int32(zz), computed))
        def _():
            y_result(zz).wait_send()

        @pl.when(among(z, jnp.int32(zz), exports))
        def _():
            for yy in range(2):
                for cc in range(n_col):
                    tile_copy(zz, yy, cc).wait_send()
            back_copy(zz).wait_send()


def body(n_row, n_col, densities, counts, coulomb, energies, vectors):
    block, depth = densities.shape
    nv = vectors.shape[1]
    line, chips = n_row // 2, n_col // 2
    plane = 2 * n_col
    chunks = 3
    bf16, f32 = jnp.bfloat16, jnp.float32
    rest = block % LANES
    vrows = nv + nv // groups_of(nv, rest)
    trows = block + block // groups_of(block, rest)
    special = any(plan(line)[1])
    vmem = pl.BlockSpec(memory_space=pltpu.VMEM)
    dma = pltpu.SemaphoreType.DMA
    wide = n_col * block
    tiles = (line, 2, n_col, trows, LANES) if special else (1, 1, 1, trows, LANES)
    kernel, prod = pl.pallas_call(
        functools.partial(exchange_kernel, n_row, n_col, chunks),
        out_shape=(
            jax.ShapeDtypeStruct((wide, n_row * block), bf16),
            jax.ShapeDtypeStruct((nv, block), f32),
        ),
        in_specs=[vmem] * 5,
        out_specs=(vmem, vmem),
        scratch_shapes=[
            pltpu.VMEM((2, n_col, block, depth), bf16),
            pltpu.VMEM((line + 1, block, depth), bf16),
            pltpu.VMEM((line, 2, block, wide), bf16),
            pltpu.VMEM((line, block, wide), bf16),
            pltpu.VMEM(tiles, bf16),
            pltpu.VMEM(tiles, bf16),
            pltpu.VMEM((line + 1, vrows, LANES), bf16),
            pltpu.VMEM((2, n_col, vrows, LANES), bf16),
            pltpu.VMEM((2, nv, wide), bf16),
            pltpu.VMEM((2, nv, wide), f32),
            pltpu.VMEM((line + 1, nv, block), f32),
            pltpu.VMEM((line, vrows, LANES), bf16),
            pltpu.VMEM((line, vrows, LANES), bf16),
            pltpu.VMEM((plane, vrows, LANES), bf16),
            pltpu.VMEM((plane, vrows, LANES), bf16),
            dma((line, chunks)), dma((line, chunks)), dma((line, chunks)),
            dma((chips, 2)), dma((chips,)), dma((2,)), dma((chips,)),
            dma((2, chips, 2)), dma((2, chips, 2)), dma((2, chips, 2)),
            dma((plane,)), dma((plane,)), dma((line,)), dma((line,)),
            dma((line,)), dma((line,)),
            dma((line, 2, n_col)), dma((line, 2, n_col)), dma((line,)), dma((line,)),
            dma((plane,)), dma((plane,)),
        ],
        compiler_params=pltpu.CompilerParams(
            collective_id=0, has_side_effects=True, vmem_limit_bytes=60 * 2**20),
    )(densities, counts[None], energies[None], vectors.T, coulomb[None])
    return (kernel.astype(f32), prod.T)


def solution(mesh):
    return jax.shard_map(
        functools.partial(body, mesh.shape["row"], mesh.shape["col"]),
        mesh=mesh,
        in_specs=(
            P(("row", "col"), None),
            P(("row", "col")),
            P(),
            P(("row", "col")),
            P(("row", "col"), None),
        ),
        out_specs=(P("row", "col"), P(("row", "col"), None)),
        check_vma=False,
    )
```

time: 83.1 us -> 72.2 us (0.87)
  the two profiles are of different devices: /device:TPU:0 before, /device:TPU:25 now
where the time goes in v1:
time: 72.2 us; the launch traced here: 72 us
  Pallas kernels  67.7 us (94%)
  other arithmetic  3.04 us (4%)
    pallas_call x1, Pallas kernels, body(): pl.pallas_call(functools.partial(exchange_kernel, n_row, n_col, chunks),...  67.7 us
    convert_element_type x1, other arithmetic, body(): return (kernel.astype(f32), prod.T)  3.04 us

profile of v1, /device:TPU:25, one launch (start us, length us, event | category | flops | bytes accessed | tf_op | source)
XLA Modules:
  0.0 72.0 jit_solution(14431118967240495740)
XLA Ops:
  0.6 67.7 %shard_map.68 = (bf16[576,1152]{1,0:T(8,128)(2,1)}, f32[64,144]{1,0:T(8,128)}) custom-call(bf16[144,3072]{1,0:T(8,128)(2,1)} %raw_ref.1, s32[1,16]{1,0:T(1,128)} %bitcast.9, f32[1,144]{1,0:T(1,128)} %bitcast.8, bf16[64,144]{1,0:T(8,128)(2,1)} %bitcast.6, f32[1,3072]{1,0:T(1,128)} %bitcast.7), custom_call_target="tpu_custom_call" | custom-call | tf_op jit(solution)/shard_map/pallas_call | solution.py:506
  68.4 0.0 copy-start
  68.4 3.0 %convert_element_type.3 = f32[576,1152]{1,0:T(8,128)} convert(bf16[576,1152]{1,0:T(8,128)(2,1)} %get-tuple-element.4) | non-fusion elementwise | flops 663552 | bytes 3981312 | tf_op jit(solution)/shard_map/convert_element_type | solution.py:541
  71.4 0.0 copy-done
  71.4 0.6 copy.8
Async XLA Ops:
  68.4 3.1 %copy-start = (f32[64,144]{1,0:T(8,128)S(1)}, f32[64,144]{1,0:T(8,128)}, u32[]{:S(2)}) copy-start(f32[64,144]{1,0:T(8,128)} %get-tuple-element.5) | copy-start | bytes 110596

commit v2 on v1

v2 whole, which is shorter than its diff:
```python
import functools
import math

import jax
import jax.numpy as jnp
from jax import lax
from jax.experimental import pallas as pl
from jax.experimental.pallas import tpu as pltpu
from jax.sharding import PartitionSpec as P

SLOT = 9
LANES = 128
MESH = pl.DeviceIdType.MESH
NT = (((1,), (1,)), ((), ()))
NN = (((1,), (0,)), ((), ()))


def pack(v, groups):
    height = v.shape[0] // groups
    tail = jnp.concatenate([v[j * height:(j + 1) * height, LANES:] for j in range(groups)], axis=1)
    spare = LANES - tail.shape[1]
    if spare:
        tail = jnp.concatenate([tail, jnp.zeros((height, spare), v.dtype)], axis=1)
    return jnp.concatenate([v[:, :LANES], tail], axis=0)


def unpack(p, rows, rest, groups):
    tail = jnp.concatenate([p[rows:, j * rest:(j + 1) * rest] for j in range(groups)], axis=0)
    return jnp.concatenate([p[:rows], tail], axis=1)


def groups_of(rows, rest):
    return max(g for g in range(1, LANES // rest + 1) if rows % g == 0 and rows // g % 8 == 0)


def plan(line):
    pairs = [(i, j) for i in range(line) for j in range(i + 1, line)]
    modes = {6: "jjbiii"}.get(len(pairs), "b" * len(pairs))
    computed = [[i] for i in range(line)]
    exports = [[] for _ in range(line)]
    high, low = list(range(line)), list(range(line))
    for (i, j), mode in zip(pairs, modes):
        if mode in "jb":
            computed[j].append(i)
            high[i] = max(high[i], j)
        if mode in "ib":
            computed[i].append(j)
            low[j] = min(low[j], i)
        if mode == "j":
            exports[j].append(i)
        if mode == "i":
            exports[i].append(j)
    special = len(pairs) == 6
    held = [special and low[i] < i and any(low[j] < i for j in range(i + 1, line)) for i in range(line)]
    if special:
        order = [[None, 3, None], [0, 3, 2], [3, 0, None], [None, 0, None]]
    else:
        order = [sorted((j for j in range(line) if j != i), key=lambda j: abs(i - j)) for i in range(line)]
    return computed, exports, high, low, held, order


def look(index, values):
    out = jnp.int32(0)
    for i, value in enumerate(values):
        out = jnp.where(index == i, jnp.int32(value), out)
    return out


def among(a, b, table):
    out = jnp.bool_(False)
    for i, row in enumerate(table):
        for j in row:
            out = out | ((a == i) & (b == j))
    return out


def exchange_kernel(n_row, n_col, chunks, parts, raw_hbm, counts_hbm, energies_hbm, vt_hbm, coulomb_hbm, out_ref, prod_ref,
                    raw_ref, counts_ref, energies_ref, vt_ref, coulomb_ref, load_sem,
                    rows, cols, buf, ysend, tsend, tland, vline, vland, vplane, q, back, bsend, bland, qsend, qland,
                    up_send, down_send, z_recv, x_send, xf_send, y_send, yf_send, sib_send, r_recv, s_recv,
                    vp_send, vp_recv, vl_send, vl_recv, yr_send, yr_recv, t_send, t_recv, b_send, b_recv,
                    q_send, q_recv):
    line, chips = n_row // 2, n_col // 2
    computed, exports, high, low, held, order = plan(line)
    special = any(exports)
    r, c = lax.axis_index("row"), lax.axis_index("col")
    z, y = r // 2, lax.rem(r, 2)
    x, core = c // 2, lax.rem(c, 2)
    other_y, other_core = 1 - y, 1 - core
    block, depth = raw_ref.shape
    half = depth // 2
    chunk = block // chunks
    lead = chunks // parts
    sub = block // parts
    nv = prod_ref.shape[0]
    rest = block % LANES
    vgroups, tgroups = groups_of(nv, rest), groups_of(sub, rest)
    place = y * n_col + c
    plane = 2 * n_col
    f32, bf16 = jnp.float32, jnp.bfloat16

    loads = [
        pltpu.make_async_copy(src, dst, load_sem.at[i])
        for i, (src, dst) in enumerate((
            (counts_hbm, counts_ref), (coulomb_hbm, coulomb_ref), (raw_hbm, raw_ref), (vt_hbm, vt_ref),
            (energies_hbm, energies_ref)))
    ]
    for load in loads:
        load.start()
    barrier = pltpu.get_barrier_semaphore()
    for step in range(1, plane):
        t = lax.rem(place + step, plane)
        pl.semaphore_signal(barrier, inc=1, device_id=(z * 2 + t // n_col, lax.rem(t, n_col)), device_id_type=MESH)
    for step in range(1, line):
        for cc in range(n_col):
            pl.semaphore_signal(barrier, inc=1, device_id=(lax.rem(z + step, line) * 2 + y, cc), device_id_type=MESH)

    for load in loads:
        load.wait()
    kpoints = counts_ref.shape[1]
    counts = counts_ref[...].astype(f32)
    row_index = lax.broadcasted_iota(jnp.int32, (block, kpoints), 0)
    kpoint = lax.broadcasted_iota(jnp.int32, (block, kpoints), 1)
    slot = row_index - SLOT * kpoint
    inside = (slot >= 0) & (slot < SLOT) & (slot.astype(f32) < counts)
    usable = jnp.sum(jnp.where(inside, 1.0, 0.0), axis=1, keepdims=True)
    d = jnp.where(usable > 0.5, raw_ref[...].astype(f32), 0.0)
    rows[y, c] = d.astype(bf16)
    cols[z] = (d * coulomb_ref[...]).astype(bf16)
    v_mine = pack(vt_ref[...].astype(f32), vgroups).astype(bf16)
    vline[z] = v_mine
    vland[y, c] = v_mine
    pl.semaphore_wait(barrier, plane - 1 + (line - 1) * n_col)

    partner = (z * 2 + other_y, c)
    sibling = (r, x * 2 + other_core)

    def remote(src, dst, send, recv, device):
        return pltpu.make_async_remote_copy(
            src_ref=src, dst_ref=dst, send_sem=send, recv_sem=recv, device_id=device, device_id_type=MESH)

    def piece(zp, ch):
        return cols.at[zp, pl.ds(ch * chunk, chunk)]

    def up(zp, ch):
        return remote(piece(zp, ch), piece(zp, ch), up_send.at[zp], z_recv.at[zp, ch], ((z + 1) * 2 + y, c))

    def down(zp, ch):
        return remote(piece(zp, ch), piece(zp, ch), down_send.at[zp], z_recv.at[zp, ch], ((z - 1) * 2 + y, c))

    def part(yy, cc, h):
        return rows.at[yy, cc, :, pl.ds(h * half, half)]

    def x_peer(step):
        return (r, lax.rem(x + step, chips) * 2 + core)

    def x_own(step, h):
        return remote(part(y, c, h), part(y, c, h), x_send, r_recv.at[y, x, h], x_peer(step))

    def x_forward(step):
        return remote(part(other_y, c, 1), part(other_y, c, 1), xf_send, r_recv.at[other_y, x, 1], x_peer(step))

    def y_own(h):
        return remote(part(y, c, h), part(y, c, h), y_send, r_recv.at[y, x, h], partner)

    def y_forward(xx):
        cc = xx * 2 + core
        return remote(part(y, cc, 0), part(y, cc, 0), yf_send, r_recv.at[y, xx, 0], partner)

    def share(yy, xx, h):
        cc = xx * 2 + core
        return remote(part(yy, cc, h), part(yy, cc, h), sib_send, s_recv.at[yy], sibling)

    def arrive(yy, xx, h):
        cc = xx * 2 + core
        remote(part(yy, cc, h), part(yy, cc, h), sib_send, r_recv.at[yy, xx, h], sibling).wait_recv()
        share(yy, xx, h).start()

    def shared(yy):
        half_plane = rows.at[yy, pl.ds(0, chips)]
        remote(half_plane, half_plane, sib_send, s_recv.at[yy], sibling).wait_recv()

    goes_up = look(z, [high[i] > i for i in range(line)]) > 0
    goes_down = look(z, [low[i] < i for i in range(line)]) > 0
    holds = look(z, held) > 0

    for ch in range(chunks):
        @pl.when(goes_up)
        def _():
            up(z, ch).start()

        @pl.when(goes_down & (~holds if ch >= lead else goes_down))
        def _():
            down(z, ch).start()
    for h in range(2):
        share(y, x, h).start()
        for step in range(1, chips):
            x_own(step, h).start()
        y_own(1 - h).start()

    def v_plane(step):
        t = lax.rem(place + step, plane)
        return remote(vline.at[z], vland.at[y, c], vp_send, vp_recv,
                      (z * 2 + t // n_col, lax.rem(t, n_col)))

    def v_line(zt):
        return remote(vline.at[z], vline.at[z], vl_send.at[zt], vl_recv.at[z], (zt * 2 + y, c))

    for step in range(1, plane):
        v_plane(step).start()
    for zt in range(line):
        @pl.when((z != zt) & among(zt, z, computed))
        def _():
            v_line(zt).start()
    q[...] = jnp.zeros_like(q)

    def z_event(h, ch, late=False):
        if not late:
            below = z - h

            @pl.when((below >= 0) & (look(below, high) >= z))
            def _():
                remote(piece(below, ch), piece(below, ch), up_send.at[0], z_recv.at[below, ch],
                       sibling).wait_recv()

                @pl.when(look(below, high) > z)
                def _():
                    up(below, ch).start()
        above = z + h
        mine = (above < line) & (look(above, low) <= z)
        if ch >= lead:
            mine = mine & ((look(above, held) > 0) == late)

        @pl.when(mine)
        def _():
            remote(piece(above, ch), piece(above, ch), down_send.at[0], z_recv.at[above, ch],
                   sibling).wait_recv()

            @pl.when(look(above, low) < z)
            def _():
                down(above, ch).start()
        if h == 1 and ch == chunks - 1 and not late:
            for later in range(lead, chunks):
                @pl.when(holds)
                def _():
                    down(z, later).start()

    def x_event(h):
        for step in range(1, chips):
            xs = lax.rem(x + chips - step, chips)
            arrive(y, xs, h)
            if h == 0:
                y_forward(xs).start()

    def y_event(h):
        arrive(other_y, x, h)
        if h == 1:
            for step in range(1, chips):
                x_forward(step).start()

    def far_event(h):
        for step in range(1, chips):
            arrive(other_y, lax.rem(x + chips - step, chips), h)

    def y_result(zi, p):
        rows_of = pl.ds(p * sub, sub)
        return remote(ysend.at[zi, rows_of], buf.at[zi, y, rows_of], yr_send.at[zi], yr_recv.at[zi], partner)

    def tile_copy(zi, yy, cc, p):
        return remote(tsend.at[zi, yy, cc, p], tland.at[z, yy, c, p], t_send.at[zi],
                      t_recv.at[z], (zi * 2 + y, cc))

    def back_copy(zi):
        return remote(bsend.at[zi], bland.at[z], b_send.at[zi], b_recv.at[z], (zi * 2 + y, c))

    def multiply(zi, near, opens=False, closes=False, first_part=0, last_part=parts, sends=True):
        yy = y if near else other_y
        low_row, high_row = first_part * sub, last_part * sub
        both = rows[yy].reshape(n_col * block, depth)
        tile = lax.dot_general(cols[zi, low_row:high_row, :], both, NT, preferred_element_type=f32)
        small = tile.astype(bf16)
        if near:
            own = zi == line
            buf[jnp.where(own, z, zi), jnp.where(own, other_y, y), low_row:high_row] = small
        else:
            ysend[zi, low_row:high_row] = small
            for p in range(first_part, last_part):
                y_result(zi, p).start()
        if special and sends:
            @pl.when(among(z, zi, exports))
            def _():
                for cc in range(n_col):
                    for p in range(first_part, last_part):
                        tsend[zi, yy, cc, p] = pack(
                            tile[(p - first_part) * sub:(p - first_part + 1) * sub, cc * block:(cc + 1) * block],
                            tgroups).astype(bf16)
                for p in range(first_part, last_part):
                    for cc in range(n_col):
                        tile_copy(zi, yy, cc, p).start()
                term = lax.dot_general(vplane[yy], small, NT, preferred_element_type=f32)
                if opens:
                    back[zi, :, low_row:high_row] = term
                else:
                    back[zi, :, low_row:high_row] += term
                if closes:
                    bsend[zi] = pack(back[zi], vgroups).astype(bf16)
                    back_copy(zi).start()
        v = unpack(vline[zi].astype(f32), nv, rest, vgroups)[:, low_row:high_row].astype(bf16)
        q[yy] += lax.dot_general(v, small, NN, preferred_element_type=f32)

    def v_wait(zi):
        remote(vline.at[zi], vline.at[zi], vl_send.at[zi], vl_recv.at[zi], sibling).wait_recv()

    ranks = len(order[0])
    rank_of = [[-1 if row[k] is None else row[k] for row in order] for k in range(ranks)]

    def ranked(k):
        zi = look(z, rank_of[k])

        @pl.when(zi >= 0)
        def _():
            v_wait(zi)
            multiply(zi, True, opens=True)

    def held_parts(first_part, last_part):
        for ch in range(max(lead, first_part * chunks // parts), last_part * chunks // parts):
            z_event(1, ch, True)
        zi = look(z, rank_of[2])

        @pl.when(zi >= 0)
        def _():
            if first_part == 0:
                v_wait(zi)
            multiply(zi, False, opens=True, first_part=first_part, last_part=last_part)
            multiply(zi, True, closes=last_part == parts, first_part=first_part, last_part=last_part)

    def first():
        multiply(z, True, sends=False)

    def second():
        others = qland.at[pl.ds(0, plane - 1)]
        remote(others, others, vp_send, vp_recv, sibling).wait_recv()
        vline[line] = vland[other_y, c]
        for yy in range(2):
            vplane[yy] = jnp.concatenate(
                [unpack(vland[yy, cc].astype(f32), nv, rest, vgroups) for cc in range(n_col)], axis=1).astype(bf16)
        cols[line] = (rows[other_y, c].astype(f32) * coulomb_ref[...]).astype(bf16)
        multiply(jnp.int32(line), True, sends=False)

    def place_computed(zz):
        @pl.when(among(z, jnp.int32(zz), computed))
        def _():
            remote(ysend.at[zz], buf.at[zz, other_y], yr_send.at[zz], yr_recv.at[zz], partner).wait_recv()
            out_ref[:, 2 * zz * block:2 * (zz + 1) * block] = (
                buf[zz].reshape(2 * block, n_col * block).astype(f32).T.astype(bf16))

    def place_imported(zz):
        @pl.when(among(jnp.int32(zz), z, exports))
        def _():
            tiles = []
            remote(tland.at[zz], tland.at[zz], t_send.at[zz], t_recv.at[zz], partner).wait_recv()
            for yy in range(2):
                t = tland[zz, yy].astype(f32).reshape(n_col * parts, tland.shape[4], LANES)
                tail = jnp.concatenate(
                    [t[:, sub:, j * rest:(j + 1) * rest] for j in range(tgroups)], axis=1)
                tiles.append(jnp.concatenate([t[:, :sub], tail], axis=2).reshape(n_col * block, block))
            out_ref[:, 2 * zz * block:2 * (zz + 1) * block] = jnp.concatenate(tiles, axis=1).astype(bf16)

    def shared_near():
        shared(y)

    def far_pair(t, carry):
        zi = jnp.where(t == 0, look(z, rank_of[0]), look(z, rank_of[1]))

        @pl.when(zi >= 0)
        def _():
            multiply(zi, False, closes=True)
        return carry

    def place_self():
        for zz in range(line):
            @pl.when(z == zz)
            def _():
                out_ref[:, 2 * zz * block:2 * (zz + 1) * block] = (
                    buf[zz].reshape(2 * block, n_col * block).astype(f32).T.astype(bf16))

    events = [(0.05 + (ch + h) / chunks + 0.1 * h, functools.partial(z_event, h, ch))
              for h in range(1, line) for ch in range(chunks)]
    events += [
        (0.61, functools.partial(x_event, 0)), (0.62, functools.partial(y_event, 1)),
        (1.11, functools.partial(x_event, 1)), (1.12, functools.partial(y_event, 0)),
        (1.61, functools.partial(far_event, 0)), (1.62, functools.partial(far_event, 1)),
    ]
    if special:
        events += [
            (1.14, shared_near), (1.18, first), (1.37, second),
            (1.38, functools.partial(ranked, 0)), (1.58, functools.partial(ranked, 1)),
            (1.73, functools.partial(shared, other_y)),
            (1.74, lambda: lax.fori_loop(0, 2, far_pair, 0)),
            (1.75, place_self),
        ]

    for _, event in sorted(events, key=lambda e: e[0]):
        event()
    if special:
        held_parts(0, parts - 1)
        held_parts(parts - 1, parts)
    else:
        shared(y)
        shared(other_y)
        first()
        second()
        place_self()

        def every(t, carry):
            zi = lax.rem(z + 1 + t, line)
            v_wait(zi)
            multiply(zi, True)
            multiply(zi, False)
            return carry

        lax.fori_loop(0, line - 1, every, 0)

    for yy in range(2):
        for cc in range(n_col):
            qsend[yy * n_col + cc] = pack(q[yy][:, cc * block:(cc + 1) * block], vgroups).astype(bf16)

    def q_copy(step):
        t = lax.rem(place + step, plane)
        return remote(qsend.at[t], qland.at[place], q_send, q_recv,
                      (z * 2 + t // n_col, lax.rem(t, n_col)))

    for step in range(1, plane):
        q_copy(step).start()

    last = look(z, rank_of[2]) if special else jnp.int32(-1)
    for zz in range(line):
        @pl.when((z != zz) & (last != zz))
        def _():
            place_computed(zz)

    answer = qsend[place].astype(f32)
    others = qland.at[pl.ds(0, plane - 1)]
    remote(others, others, q_send, q_recv, sibling).wait_recv()
    for step in range(1, plane):
        answer += qland[lax.rem(place + step, plane)].astype(f32)
    back[line] = unpack(answer, nv, rest, vgroups)
    if special:
        for zz in range(line):
            place_imported(zz)
    for zz in range(line):
        @pl.when(among(jnp.int32(zz), z, exports))
        def _():
            remote(bsend.at[0], bland.at[zz], b_send.at[0], b_recv.at[zz], sibling).wait_recv()
            back[line] += unpack(bland[zz].astype(f32), nv, rest, vgroups)
    lane_slot = (lax.broadcasted_iota(jnp.int32, (kpoints, block), 1)
                 - SLOT * lax.broadcasted_iota(jnp.int32, (kpoints, block), 0))
    mine = jnp.where((lane_slot >= 0) & (lane_slot < SLOT), 1.0, 0.0)
    limit = lax.dot_general(jnp.broadcast_to(counts, (8, kpoints)), mine, NN, preferred_element_type=f32)[:1]
    lane_slot = lax.rem(lax.broadcasted_iota(jnp.int32, (1, block), 1), SLOT).astype(f32)
    diagonal = jnp.where(lane_slot + 0.5 < limit, energies_ref[...], 0.0)
    prod_ref[...] = back[line] + diagonal * vt_ref[...].astype(f32)

    if special:
        for zz in range(line):
            if zz in rank_of[2]:
                @pl.when(last == zz)
                def _():
                    place_computed(zz)

    def sent(ref, sem):
        remote(ref, ref, sem, load_sem.at[0], sibling).wait_send()

    for zp in range(line):
        @pl.when((zp <= z) & (high[zp] > z))
        def _():
            sent(cols.at[zp], up_send.at[zp])

        @pl.when((zp >= z) & (low[zp] < z))
        def _():
            sent(cols.at[zp], down_send.at[zp])
    sent(rows.at[0, 0], y_send)
    sent(rows.at[0, pl.ds(0, chips - 1)], x_send)
    sent(rows.at[0, pl.ds(0, chips - 1), :, pl.ds(0, half)], xf_send)
    sent(rows.at[0, pl.ds(0, chips - 1), :, pl.ds(0, half)], yf_send)
    sent(rows.at[0], sib_send)
    sent(qland.at[pl.ds(0, plane - 1)], vp_send)
    sent(qland.at[pl.ds(0, plane - 1)], q_send)
    for zz in range(line):
        @pl.when((z != zz) & among(jnp.int32(zz), z, computed))
        def _():
            v_line(zz).wait_send()

        @pl.when((z != zz) & among(z, jnp.int32(zz), computed))
        def _():
            sent(ysend.at[zz], yr_send.at[zz])

        @pl.when(among(z, jnp.int32(zz), exports))
        def _():
            sent(tsend.at[zz], t_send.at[zz])
            back_copy(zz).wait_send()


def body(n_row, n_col, densities, counts, coulomb, energies, vectors):
    block, depth = densities.shape
    nv = vectors.shape[1]
    line, chips = n_row // 2, n_col // 2
    plane = 2 * n_col
    chunks, parts = 9, 3
    bf16, f32 = jnp.bfloat16, jnp.float32
    rest = block % LANES
    vrows = nv + nv // groups_of(nv, rest)
    trows = block // parts + block // parts // groups_of(block // parts, rest)
    special = any(plan(line)[1])
    vmem = pl.BlockSpec(memory_space=pltpu.VMEM)
    dma = pltpu.SemaphoreType.DMA
    wide = n_col * block
    tiles = (line, 2, n_col, parts, trows, LANES) if special else (1, 1, 1, 1, trows, LANES)
    scratch = [
        pltpu.VMEM((block, depth), bf16),
        pltpu.VMEM((1, counts.shape[0]), jnp.int32),
        pltpu.VMEM((1, block), f32),
        pltpu.VMEM((nv, block), bf16),
        pltpu.VMEM((1, depth), f32),
        dma((5,)),
        pltpu.VMEM((2, n_col, block, depth), bf16),
        pltpu.VMEM((line + 1, block, depth), bf16),
        pltpu.VMEM((line, 2, block, wide), bf16),
        pltpu.VMEM((line, block, wide), bf16),
        pltpu.VMEM(tiles, bf16),
        pltpu.VMEM(tiles, bf16),
        pltpu.VMEM((line + 1, vrows, LANES), bf16),
        pltpu.VMEM((2, n_col, vrows, LANES), bf16),
        pltpu.VMEM((2, nv, wide), bf16),
        pltpu.VMEM((2, nv, wide), f32),
        pltpu.VMEM((line + 1, nv, block), f32),
        pltpu.VMEM((line, vrows, LANES), bf16),
        pltpu.VMEM((line, vrows, LANES), bf16),
        pltpu.VMEM((plane, vrows, LANES), bf16),
        pltpu.VMEM((plane, vrows, LANES), bf16),
        dma((line,)), dma((line,)), dma((line, chunks)),
        dma, dma, dma, dma, dma, dma((2, chips, 2)), dma((2,)),
        dma, dma, dma((line,)), dma((line,)),
        dma((line,)), dma((line,)), dma((line,)), dma((line,)), dma((line,)), dma((line,)),
        dma, dma,
    ]
    held = sum(math.prod(ref.shape[:-1]) * -(-ref.shape[-1] // LANES) * LANES * jnp.dtype(ref.dtype).itemsize
               for ref in scratch if getattr(ref, 'dtype', None) in (bf16, f32))
    kernel, prod = pl.pallas_call(
        functools.partial(exchange_kernel, n_row, n_col, chunks, parts),
        out_shape=(
            jax.ShapeDtypeStruct((wide, n_row * block), bf16),
            jax.ShapeDtypeStruct((nv, block), f32),
        ),
        in_specs=[pl.BlockSpec(memory_space=pltpu.MemorySpace.HBM)] * 5,
        out_specs=(vmem, vmem),
        scratch_shapes=scratch,
        compiler_params=pltpu.CompilerParams(
            collective_id=0, has_side_effects=True, vmem_limit_bytes=min(60 * 2**20, held + held // 8 + 6 * 2**20)),
    )(*(pltpu.with_memory_space_constraint(operand, pltpu.MemorySpace.HBM)
        for operand in (densities, counts[None], energies[None], vectors.T, coulomb[None])))
    return (kernel.astype(f32), prod.T)


def solution(mesh):
    return jax.shard_map(
        functools.partial(body, mesh.shape["row"], mesh.shape["col"]),
        mesh=mesh,
        in_specs=(
            P(("row", "col"), None),
            P(("row", "col")),
            P(),
            P(("row", "col")),
            P(("row", "col"), None),
        ),
        out_specs=(P("row", "col"), P(("row", "col"), None)),
        check_vma=False,
    )
```

time: 72.2 us -> 61.7 us (0.85)
  the two profiles are of different devices: /device:TPU:25 before, /device:TPU:0 now
where the time goes in v2:
time: 61.7 us; the launch traced here: 61.6 us
  Pallas kernels  58.6 us (95%)
  other arithmetic  1.69 us (3%)
  between operations  0.64 us (1%)
  local copies, waits for them, and re-layouts  0.63 us (1%)
    pallas_call x1, Pallas kernels, body(): pl.pallas_call(functools.partial(exchange_kernel, n_row, n_col, chunks, p...  58.6 us
    convert_element_type x1, other arithmetic, body(): return (kernel.astype(f32), prod.T)  1.69 us

profile of v2, /device:TPU:0, one launch (start us, length us, event | category | flops | bytes accessed | tf_op | source)
XLA Modules:
  0.0 61.6 jit_solution(5720804103540430256)
XLA Ops:
  0.6 58.6 %shard_map.68 = (bf16[576,1152]{1,0:T(8,128)(2,1)S(1)}, f32[64,144]{1,0:T(8,128)S(1)}) custom-call(bf16[144,3072]{1,0:T(8,128)(2,1)} %raw_hbm.1, s32[1,16]{1,0:T(1,128)} %bitcast.9, f32[1,144]{1,0:T(1,128)} %bitcast.8, bf16[64,144]{1,0:T(8,128)(2,1)} %bitcast.6, f32[1,3072]{1,0:T(1,128)} %bitcast.7), custom_call_target="tpu_custom_call" | custom-call | tf_op jit(solution)/shard_map/pallas_call | solution.py:549
  59.3 1.7 %convert_element_type.3 = f32[576,1152]{1,0:T(8,128)} convert(bf16[576,1152]{1,0:T(8,128)(2,1)S(1)} %get-tuple-element.4) | non-fusion elementwise | flops 663552 | bytes 3981312 | tf_op jit(solution)/shard_map/convert_element_type | solution.py:562
  60.9 0.6 %copy.8 = f32[144,64]{0,1:T(8,128)} copy(f32[144,64]{0,1:T(8,128)S(1)} %bitcast.5) | data formatting | bytes 73728

commit v3 on v2

v3 whole, which is shorter than its diff:
```python
import functools
import math

import jax
import jax.numpy as jnp
from jax import lax
from jax.experimental import pallas as pl
from jax.experimental.pallas import tpu as pltpu
from jax.sharding import PartitionSpec as P

SLOT = 9
LANES = 128
COPIES = 4
MESH = pl.DeviceIdType.MESH
NT = (((1,), (1,)), ((), ()))
NN = (((1,), (0,)), ((), ()))


def pack(v, groups):
    height = v.shape[0] // groups
    tail = jnp.concatenate([v[j * height:(j + 1) * height, LANES:] for j in range(groups)], axis=1)
    spare = LANES - tail.shape[1]
    if spare:
        tail = jnp.concatenate([tail, jnp.zeros((height, spare), v.dtype)], axis=1)
    return jnp.concatenate([v[:, :LANES], tail], axis=0)


def unpack(p, rows, rest, groups):
    tail = jnp.concatenate([p[rows:, j * rest:(j + 1) * rest] for j in range(groups)], axis=0)
    return jnp.concatenate([p[:rows], tail], axis=1)


def groups_of(rows, rest):
    return max(g for g in range(1, LANES // rest + 1) if rows % g == 0 and rows // g % 8 == 0)


def plan(line):
    pairs = [(i, j) for i in range(line) for j in range(i + 1, line)]
    modes = {6: "jjbiii"}.get(len(pairs), "b" * len(pairs))
    computed = [[i] for i in range(line)]
    exports = [[] for _ in range(line)]
    high, low = list(range(line)), list(range(line))
    for (i, j), mode in zip(pairs, modes):
        if mode in "jb":
            computed[j].append(i)
            high[i] = max(high[i], j)
        if mode in "ib":
            computed[i].append(j)
            low[j] = min(low[j], i)
        if mode == "j":
            exports[j].append(i)
        if mode == "i":
            exports[i].append(j)
    special = len(pairs) == 6
    held = [special and low[i] < i and any(low[j] < i for j in range(i + 1, line)) for i in range(line)]
    order = [[None, 3], [2, None], [None, None], [None, 0]] if special else [[None, None]] * line
    slots = [0, 2, 3, 1] if special else list(range(line))
    return computed, exports, high, low, held, order, slots


def look(index, values):
    out = jnp.int32(0)
    for i, value in enumerate(values):
        out = jnp.where(index == i, jnp.int32(value), out)
    return out


def among(a, b, table):
    out = jnp.bool_(False)
    for i, row in enumerate(table):
        for j in row:
            out = out | ((a == i) & (b == j))
    return out


def exchange_kernel(n_row, n_col, chunks, parts, raw_hbm, counts_hbm, energies_hbm, vt_hbm, coulomb_hbm, out_ref, prod_ref,
                    raw_ref, counts_ref, energies_ref, vt_ref, coulomb_ref, load_sem,
                    rows, w_ref, cols, buf, tsend, tland, yland, vline, vland, vplane, vchip, q, qfar, back, bsend, bland, qsend, qland,
                    up_send, down_send, z_recv, x_send, xf_send, y_send, yf_send, sib_send, r_recv, s_recv,
                    vp_send, vp_recv, vl_send, vl_recv, yr_send, yr_recv, t_send, t_recv, b_send, b_recv,
                    q_send, q_recv):
    line, chips = n_row // 2, n_col // 2
    computed, exports, high, low, held, order, slots = plan(line)
    special = any(exports)
    r, c = lax.axis_index("row"), lax.axis_index("col")
    z, y = line - 1 - r // 2, lax.rem(r, 2)
    x, core = c // 2, lax.rem(c, 2)
    other_y, other_core = 1 - y, 1 - core
    block, depth = raw_ref.shape
    half = depth // 2
    chunk = block // chunks
    lead = chunks // 4
    sub = block // parts
    nv = prod_ref.shape[0]
    rest = block % LANES
    vgroups, tgroups = groups_of(nv, rest), groups_of(sub, rest)
    place = y * n_col + c
    plane = 2 * n_col
    f32, bf16 = jnp.float32, jnp.bfloat16

    loads = [
        pltpu.make_async_copy(src, dst, load_sem.at[i])
        for i, (src, dst) in enumerate((
            (counts_hbm, counts_ref), (coulomb_hbm, coulomb_ref), (raw_hbm, raw_ref), (vt_hbm, vt_ref),
            (energies_hbm, energies_ref)))
    ]
    for load in loads:
        load.start()
    def row_of(zp, yy):
        return (line - 1 - zp) * 2 + yy

    barrier = pltpu.get_barrier_semaphore()
    for step in range(1, plane):
        t = lax.rem(place + step, plane)
        pl.semaphore_signal(barrier, inc=1, device_id=(row_of(z, t // n_col), lax.rem(t, n_col)), device_id_type=MESH)
    for step in range(1, line):
        for cc in range(n_col):
            pl.semaphore_signal(barrier, inc=1, device_id=(row_of(lax.rem(z + step, line), y), cc), device_id_type=MESH)

    for load in loads:
        load.wait()
    kpoints = counts_ref.shape[1]
    counts = counts_ref[...].astype(f32)
    row_index = lax.broadcasted_iota(jnp.int32, (block, kpoints), 0)
    kpoint = lax.broadcasted_iota(jnp.int32, (block, kpoints), 1)
    slot = row_index - SLOT * kpoint
    inside = (slot >= 0) & (slot < SLOT) & (slot.astype(f32) < counts)
    usable = jnp.sum(jnp.where(inside, 1.0, 0.0), axis=1, keepdims=True)
    d = jnp.where(usable > 0.5, raw_ref[...].astype(f32), 0.0)
    rows[y, c] = d.astype(bf16)
    w_ref[0] = (d * coulomb_ref[...]).astype(bf16)
    v_mine = pack(vt_ref[...].astype(f32), vgroups).astype(bf16)
    vline[z] = v_mine
    vland[y, c] = v_mine
    pl.semaphore_wait(barrier, plane - 1 + (line - 1) * n_col)

    partner = (row_of(z, other_y), c)
    sibling = (r, x * 2 + other_core)

    def remote(src, dst, send, recv, device):
        return pltpu.make_async_remote_copy(
            src_ref=src, dst_ref=dst, send_sem=send, recv_sem=recv, device_id=device, device_id_type=MESH)

    def slot_of(zp):
        return look(zp, slots)

    def piece(zp, ch):
        return cols.at[slot_of(zp), pl.ds(ch * chunk, chunk)]

    def relay(zp, ch, step):
        send = up_send if step > 0 else down_send
        src = piece(zp, ch)
        remote(src, src, send.at[zp], z_recv.at[zp, ch], (row_of(z + step, y), c)).start()

    def launch(ch, step):
        send = up_send if step > 0 else down_send
        remote(w_ref.at[0, pl.ds(ch * chunk, chunk)], piece(z, ch), send.at[z], z_recv.at[z, ch],
               (row_of(z + step, y), c)).start()

    def part(yy, cc, h):
        return rows.at[yy, cc, :, pl.ds(h * half, half)]

    def x_peer(step):
        return (r, lax.rem(x + step, chips) * 2 + core)

    def x_own(step, h):
        return remote(part(y, c, h), part(y, c, h), x_send, r_recv.at[y, x, h], x_peer(step))

    def x_forward(step):
        return remote(part(other_y, c, 1), part(other_y, c, 1), xf_send, r_recv.at[other_y, x, 1], x_peer(step))

    def y_own(h):
        return remote(part(y, c, h), part(y, c, h), y_send, r_recv.at[y, x, h], partner)

    def y_forward(xx):
        cc = xx * 2 + core
        return remote(part(y, cc, 0), part(y, cc, 0), yf_send, r_recv.at[y, xx, 0], partner)

    def share(yy, xx, h, group):
        cc = xx * 2 + core
        return remote(part(yy, cc, h), part(yy, cc, h), sib_send, s_recv.at[group], sibling)

    def arrive(yy, xx, h, group):
        cc = xx * 2 + core
        remote(part(yy, cc, h), part(yy, cc, h), sib_send, r_recv.at[yy, xx, h], sibling).wait_recv()
        share(yy, xx, h, group).start()

    def shared(group):
        blocks = rows.at[0, pl.ds(0, (chips, 1, chips - 1)[group])]
        remote(blocks, blocks, sib_send, s_recv.at[group], sibling).wait_recv()

    goes_up = look(z, [high[i] > i for i in range(line)]) > 0
    goes_down = look(z, [low[i] < i for i in range(line)]) > 0
    holds = look(z, held) > 0

    for ch in range(chunks):
        @pl.when(goes_up)
        def _():
            launch(ch, 1)

        @pl.when(goes_down & (~holds if ch >= lead else goes_down))
        def _():
            launch(ch, -1)
    for h in range(2):
        share(y, x, h, 0).start()
        for step in range(1, chips):
            x_own(step, h).start()
        y_own(1 - h).start()

    def v_plane(step):
        t = lax.rem(place + step, plane)
        return remote(vline.at[z], vland.at[y, c], vp_send, vp_recv,
                      (row_of(z, t // n_col), lax.rem(t, n_col)))

    def v_line(zt):
        return remote(vline.at[z], vline.at[z], vl_send.at[zt], vl_recv.at[z], (row_of(zt, y), c))

    for step in range(1, plane):
        v_plane(step).start()
    for zt in range(line):
        @pl.when((z != zt) & among(zt, z, computed))
        def _():
            v_line(zt).start()
    q[...] = jnp.zeros_like(q)
    qfar[...] = jnp.zeros_like(qfar)

    def z_event(h, ch, late=False):
        if not late:
            below = z - h

            @pl.when((below >= 0) & (look(below, high) >= z))
            def _():
                remote(piece(below, ch), piece(below, ch), up_send.at[0], z_recv.at[below, ch],
                       sibling).wait_recv()

                @pl.when(look(below, high) > z)
                def _():
                    relay(below, ch, 1)
        above = z + h
        mine = (above < line) & (look(above, low) <= z)
        if ch >= lead:
            mine = mine & ((look(above, held) > 0) == late)

        @pl.when(mine)
        def _():
            remote(piece(above, ch), piece(above, ch), down_send.at[0], z_recv.at[above, ch],
                   sibling).wait_recv()

            @pl.when(look(above, low) < z)
            def _():
                relay(above, ch, -1)
        if h == 1 and ch == chunks - 1 and not late:
            for later in range(lead, chunks):
                @pl.when(holds)
                def _():
                    launch(later, -1)

    def x_event(h):
        for step in range(1, chips):
            xs = lax.rem(x + chips - step, chips)
            arrive(y, xs, h, 0)
            if h == 0:
                y_forward(xs).start()

    def y_event(h):
        arrive(other_y, x, h, 1)
        if h == 1:
            for step in range(1, chips):
                x_forward(step).start()

    def far_event(h):
        for step in range(1, chips):
            arrive(other_y, lax.rem(x + chips - step, chips), h, 2)

    def y_result(zi, cc, first_part=0, last_part=parts):
        mine = pl.ds(first_part, last_part - first_part)
        return remote(tsend.at[zi, other_y, cc, mine], yland.at[zi, cc, mine], yr_send.at[zi], yr_recv.at[zi], partner)

    def tile_copy(zi, yy, cc, first_part=0, last_part=parts):
        mine = pl.ds(first_part, last_part - first_part)
        return remote(tsend.at[zi, yy, cc, mine], tland.at[z, yy, c, mine], t_send.at[zi], t_recv.at[z],
                      (row_of(zi, y), cc))

    def back_copy(zi):
        return remote(bsend.at[zi], bland.at[z], b_send.at[zi], b_recv.at[z], (row_of(zi, y), c))

    def emit(zi, near, tile, chip=None, opens=False, closes=False, first_part=0, last_part=parts, sends=True,
             starts=True):
        yy = y if near else other_y
        low_row, high_row = first_part * sub, last_part * sub
        small = tile.astype(bf16)
        mine = range(n_col) if chip is None else [chip * 2, chip * 2 + 1]
        if near:
            buf[zi, low_row:high_row] = small
        if sends or not near:
            for i, cc in enumerate(mine):
                for p in range(first_part, last_part):
                    tsend[zi, yy, cc, p] = pack(
                        tile[(p - first_part) * sub:(p - first_part + 1) * sub, i * block:(i + 1) * block],
                        tgroups).astype(bf16)
        if not near:
            for cc in mine:
                y_result(zi, cc, first_part, last_part).start()
        v = unpack(vline[zi].astype(f32), nv, rest, vgroups)[:, low_row:high_row].astype(bf16)
        if sends:
            for cc in mine if starts else ():
                tile_copy(zi, yy, cc, first_part, last_part).start()
            vectors = vplane[yy] if chip is None else vchip[chip]
            term = lax.dot_general(vectors, small, NT, preferred_element_type=f32)
            if opens:
                back[zi, :, low_row:high_row] = term
            else:
                back[zi, :, low_row:high_row] += term
            if closes:
                bsend[zi] = pack(back[zi], vgroups).astype(bf16)
                back_copy(zi).start()
        term = lax.dot_general(v, small, NN, preferred_element_type=f32)
        if near:
            q[...] += term
        elif chip is None:
            for xx in range(chips):
                qfar[xx] += term[:, 2 * xx * block:2 * (xx + 1) * block]
        else:
            qfar[chip] += term

    def plane_rows(yy, chip=None):
        if chip is None:
            return rows[yy].reshape(n_col * block, depth)
        return rows[yy, pl.ds(chip * 2, 2)].reshape(2 * block, depth)

    def multiply(zi, near, first_part=0, last_part=parts, **how):
        tile = lax.dot_general(cols[slot_of(zi), first_part * sub:last_part * sub, :], plane_rows(y if near else other_y),
                               NT, preferred_element_type=f32)
        emit(zi, near, tile, first_part=first_part, last_part=last_part, **how)

    def ends(near, chip=None, opens=False, closes=False):
        @pl.when((z > 0) & (z < line - 1))
        def _():
            if opens:
                v_wait(0)
                v_wait(line - 1)
            tile = lax.dot_general(cols[0:2].reshape(2 * block, depth), plane_rows(y if near else other_y, chip), NT,
                                   preferred_element_type=f32)
            for i, zi in enumerate((0, line - 1)):
                emit(zi, near, tile[i * block:(i + 1) * block], chip=chip, opens=opens, closes=closes,
                     starts=closes or zi == 0)

    def late_tiles():
        @pl.when((z > 0) & (z < line - 1))
        def _():
            for i in range(2):
                tile_copy(line - 1, other_y, x * 2 + i).start()
            for cc in range(n_col):
                tile_copy(line - 1, y, cc).start()

    def v_wait(zi):
        remote(vline.at[zi], vline.at[zi], vl_send.at[zi], vl_recv.at[zi], sibling).wait_recv()

    rank_of = [[-1 if row[k] is None else row[k] for row in order] for k in range(2)]

    def held_parts(first_part, last_part):
        for ch in range(max(lead, first_part * chunks // parts), last_part * chunks // parts):
            z_event(1, ch, True)
        zi = look(z, rank_of[0])

        @pl.when(zi >= 0)
        def _():
            if first_part == 0:
                v_wait(zi)
            multiply(zi, False, opens=True, first_part=first_part, last_part=last_part)
            multiply(zi, True, closes=last_part == parts, first_part=first_part, last_part=last_part)

    def plane_vectors():
        others = qland.at[pl.ds(0, plane - 1)]
        remote(others, others, vp_send, vp_recv, sibling).wait_recv()
        for yy in range(2):
            vplane[yy] = jnp.concatenate(
                [unpack(vland[yy, cc].astype(f32), nv, rest, vgroups) for cc in range(n_col)], axis=1).astype(bf16)
        for xx in range(chips):
            vchip[xx] = jnp.concatenate(
                [unpack(vland[other_y, 2 * xx + i].astype(f32), nv, rest, vgroups) for i in range(2)], axis=1).astype(bf16)
    def own_plane():
        w_ref[1] = (rows[other_y, c].astype(f32) * coulomb_ref[...]).astype(bf16)
        tile = lax.dot_general(w_ref[...].reshape(2 * block, depth), plane_rows(y), NT, preferred_element_type=f32)
        small = tile.astype(bf16)
        buf[z] = small[:block]
        buf[line] = small[block:]
        v = jnp.concatenate(
            [unpack(ref.astype(f32), nv, rest, vgroups) for ref in (vline[z], vland[other_y, c])], axis=1).astype(bf16)
        q[...] += lax.dot_general(v, small, NN, preferred_element_type=f32)

    def arrange(ref):
        t = ref[...].astype(f32).reshape(n_col * parts, ref.shape[-2], LANES)
        tail = jnp.concatenate([t[:, sub:, j * rest:(j + 1) * rest] for j in range(tgroups)], axis=1)
        return jnp.concatenate([t[:, :sub], tail], axis=2).reshape(n_col * block, block)

    def lanes_of(zz):
        return slice(2 * (line - 1 - zz) * block, 2 * (line - zz) * block)

    def place_pair(zz, near, far):
        first, second = jnp.where(y == 0, near, far), jnp.where(y == 0, far, near)
        out_ref[:, lanes_of(zz)] = jnp.concatenate([first, second], axis=0).T

    def place_computed(zz):
        @pl.when(among(z, jnp.int32(zz), computed))
        def _():
            remote(yland.at[zz], yland.at[zz], yr_send.at[zz], yr_recv.at[zz], partner).wait_recv()
            t = arrange(yland.at[zz]).reshape(n_col, block, block)
            far = jnp.concatenate([t[cc] for cc in range(n_col)], axis=1)
            place_pair(zz, buf[zz].astype(f32), far)

    def place_imported(zz):
        @pl.when(among(jnp.int32(zz), z, exports))
        def _():
            remote(tland.at[zz], tland.at[zz], t_send.at[zz], t_recv.at[zz], partner).wait_recv()
            out_ref[:, lanes_of(zz)] = jnp.concatenate(
                [arrange(tland.at[zz, yy]) for yy in range(2)], axis=1)

    def edge(first_part, last_part):
        zi = look(z, rank_of[1])

        @pl.when(zi >= 0)
        def _():
            if first_part == 0:
                v_wait(zi)
            multiply(zi, False, first_part, last_part, sends=False)
            multiply(zi, True, first_part, last_part, sends=False)

    def place_self():
        for zz in range(line):
            @pl.when(z == zz)
            def _():
                place_pair(zz, buf[zz].astype(f32), buf[line].astype(f32))

    def own_at(outer):
        at_end = (z == 0) | (z == line - 1)

        @pl.when(at_end if outer else ~at_end)
        def _():
            own_plane()
            place_self()

    def z_time(h, ch):
        if special and h == line - 1:
            return 1.8 if ch < (parts - 1) * chunks // parts else 1.82
        return 0.05 + (ch + h) / chunks + 0.1 * h + (0.1 if h > 1 else 0.0)

    events = [(z_time(h, ch), functools.partial(z_event, h, ch)) for h in range(1, line) for ch in range(chunks)]
    events += [
        (0.61, functools.partial(x_event, 0)), (0.62, functools.partial(y_event, 1)),
        (1.11, functools.partial(x_event, 1)), (1.12, functools.partial(y_event, 0)),
        (1.61, functools.partial(far_event, 0)), (1.62, functools.partial(far_event, 1)),
    ]
    if special:
        events += [
            (1.18, functools.partial(shared, 0)), (1.499, functools.partial(shared, 1)), (1.185, plane_vectors), (1.19, lambda: own_at(True)), (1.5, lambda: ends(False, x, opens=True)), (1.501, functools.partial(ends, True)),
            (1.503, late_tiles), (1.73, functools.partial(shared, 2)), (1.74, lambda: ends(False, 1 - x, closes=True)),
            (1.81, lambda: edge(0, parts - 1)), (1.83, lambda: edge(parts - 1, parts)),
        ]

    for _, event in sorted(events, key=lambda e: e[0]):
        event()
    if special:
        held_parts(0, parts - 1)
        own_at(False)
        held_parts(parts - 1, parts)
    else:
        for group in range(3):
            shared(group)
        plane_vectors()
        own_plane()
        place_self()

        def every(t, carry):
            zi = lax.rem(z + 1 + t, line)
            v_wait(zi)
            multiply(zi, True, sends=False)
            multiply(zi, False, sends=False)
            return carry

        lax.fori_loop(0, line - 1, every, 0)

    for cc in range(n_col):
        qsend[y * n_col + cc] = pack(q[:, cc * block:(cc + 1) * block], vgroups).astype(bf16)
        low_lane = cc % 2 * block
        qsend[other_y * n_col + cc] = pack(qfar[cc // 2, :, low_lane:low_lane + block], vgroups).astype(bf16)

    def q_copy(step):
        t = lax.rem(place + step, plane)
        return remote(qsend.at[t], qland.at[place], q_send, q_recv,
                      (row_of(z, t // n_col), lax.rem(t, n_col)))

    for step in range(1, plane):
        q_copy(step).start()

    last = look(z, rank_of[0])
    for zz in range(line):
        @pl.when((z != zz) & (last != zz))
        def _():
            place_computed(zz)

    if special:
        for zz in range(line):
            place_imported(zz)
        for zz in range(line):
            if zz in rank_of[0]:
                @pl.when(last == zz)
                def _():
                    place_computed(zz)

    answer = qsend[place].astype(f32)
    others = qland.at[pl.ds(0, plane - 1)]
    remote(others, others, q_send, q_recv, sibling).wait_recv()
    for step in range(1, plane):
        answer += qland[lax.rem(place + step, plane)].astype(f32)
    back[line] = unpack(answer, nv, rest, vgroups)
    for zz in range(line):
        @pl.when(among(jnp.int32(zz), z, exports))
        def _():
            remote(bsend.at[0], bland.at[zz], b_send.at[0], b_recv.at[zz], sibling).wait_recv()
            back[line] += unpack(bland[zz].astype(f32), nv, rest, vgroups)
    lane_slot = (lax.broadcasted_iota(jnp.int32, (kpoints, block), 1)
                 - SLOT * lax.broadcasted_iota(jnp.int32, (kpoints, block), 0))
    mine = jnp.where((lane_slot >= 0) & (lane_slot < SLOT), 1.0, 0.0)
    limit = lax.dot_general(jnp.broadcast_to(counts, (8, kpoints)), mine, NN, preferred_element_type=f32)[:1]
    lane_slot = lax.rem(lax.broadcasted_iota(jnp.int32, (1, block), 1), SLOT).astype(f32)
    diagonal = jnp.where(lane_slot + 0.5 < limit, energies_ref[...], 0.0)
    prod_ref[...] = back[line] + diagonal * vt_ref[...].astype(f32)

    def sent(ref, sem):
        remote(ref, ref, sem, load_sem.at[0], sibling).wait_send()

    for zp in range(line):
        @pl.when((zp <= z) & (high[zp] > z))
        def _():
            sent(cols.at[zp], up_send.at[zp])

        @pl.when((zp >= z) & (low[zp] < z))
        def _():
            sent(cols.at[zp], down_send.at[zp])
    sent(rows.at[0, 0], y_send)
    sent(rows.at[0, pl.ds(0, chips - 1)], x_send)
    sent(rows.at[0, pl.ds(0, chips - 1), :, pl.ds(0, half)], xf_send)
    sent(rows.at[0, pl.ds(0, chips - 1), :, pl.ds(0, half)], yf_send)
    sent(rows.at[0], sib_send)
    sent(qland.at[pl.ds(0, plane - 1)], vp_send)
    sent(qland.at[pl.ds(0, plane - 1)], q_send)
    for zz in range(line):
        @pl.when((z != zz) & among(jnp.int32(zz), z, computed))
        def _():
            v_line(zz).wait_send()

        @pl.when((z != zz) & among(z, jnp.int32(zz), computed))
        def _():
            sent(yland.at[zz], yr_send.at[zz])

        @pl.when(among(z, jnp.int32(zz), exports))
        def _():
            sent(tsend.at[zz], t_send.at[zz])
            back_copy(zz).wait_send()


def write_kernel(kernel_ref, prod_ref, kernel_out, prod_out, sem):
    height = kernel_ref.shape[0] // COPIES
    copies = [pltpu.make_async_copy(prod_ref, prod_out, sem.at[COPIES])]
    for i in range(COPIES):
        part = pl.ds(i * height, height)
        copies.append(pltpu.make_async_copy(kernel_ref.at[part], kernel_out.at[part], sem.at[i]))
    for copy in copies:
        copy.start()
    for copy in copies:
        copy.wait()


def body(n_row, n_col, densities, counts, coulomb, energies, vectors):
    block, depth = densities.shape
    nv = vectors.shape[1]
    line, chips = n_row // 2, n_col // 2
    plane = 2 * n_col
    chunks, parts = 9, 3
    bf16, f32 = jnp.bfloat16, jnp.float32
    rest = block % LANES
    vrows = nv + nv // groups_of(nv, rest)
    trows = block // parts + block // parts // groups_of(block // parts, rest)
    special = any(plan(line)[1])
    vmem = pl.BlockSpec(memory_space=pltpu.VMEM)
    dma = pltpu.SemaphoreType.DMA
    wide = n_col * block
    scratch = [
        pltpu.VMEM((block, depth), bf16),
        pltpu.VMEM((1, counts.shape[0]), jnp.int32),
        pltpu.VMEM((1, block), f32),
        pltpu.VMEM((nv, block), bf16),
        pltpu.VMEM((1, depth), f32),
        dma((5,)),
        pltpu.VMEM((2, n_col, block, depth), bf16),
        pltpu.VMEM((2, block, depth), bf16),
        pltpu.VMEM((line, block, depth), bf16),
        pltpu.VMEM((line + 1, block, wide), bf16),
        pltpu.VMEM((line, 2, n_col, parts, trows, LANES), bf16),
        pltpu.VMEM((line if special else 1, 2, n_col, parts, trows, LANES), bf16),
        pltpu.VMEM((line, n_col, parts, trows, LANES), bf16),
        pltpu.VMEM((line, vrows, LANES), bf16),
        pltpu.VMEM((2, n_col, vrows, LANES), bf16),
        pltpu.VMEM((2, nv, wide), bf16),
        pltpu.VMEM((chips, nv, 2 * block), bf16),
        pltpu.VMEM((nv, wide), f32),
        pltpu.VMEM((chips, nv, 2 * block), f32),
        pltpu.VMEM((line + 1, nv, block), f32),
        pltpu.VMEM((line, vrows, LANES), bf16),
        pltpu.VMEM((line, vrows, LANES), bf16),
        pltpu.VMEM((plane, vrows, LANES), bf16),
        pltpu.VMEM((plane, vrows, LANES), bf16),
        dma((line,)), dma((line,)), dma((line, chunks)),
        dma, dma, dma, dma, dma, dma((2, chips, 2)), dma((3,)),
        dma, dma, dma((line,)), dma((line,)),
        dma((line,)), dma((line,)), dma((line,)), dma((line,)), dma((line,)), dma((line,)),
        dma, dma,
    ]
    held = sum(math.prod(ref.shape[:-1]) * -(-ref.shape[-1] // LANES) * LANES * jnp.dtype(ref.dtype).itemsize
               for ref in scratch if getattr(ref, 'dtype', None) in (bf16, f32))
    result = wide * n_row * block * 4
    kernel, prod = pl.pallas_call(
        functools.partial(exchange_kernel, n_row, n_col, chunks, parts),
        out_shape=(
            jax.ShapeDtypeStruct((wide, n_row * block), f32),
            jax.ShapeDtypeStruct((nv, block), f32),
        ),
        in_specs=[pl.BlockSpec(memory_space=pltpu.MemorySpace.HBM)] * 5,
        out_specs=(vmem, vmem),
        scratch_shapes=scratch,
        compiler_params=pltpu.CompilerParams(
            collective_id=0, has_side_effects=True, vmem_limit_bytes=min(60 * 2**20, held + held // 8 + result + 4 * 2**20)),
    )(*(pltpu.with_memory_space_constraint(operand, pltpu.MemorySpace.HBM)
        for operand in (densities, counts[None], energies[None], vectors.T, coulomb[None])))
    kernel, prod = pl.pallas_call(
        write_kernel,
        out_shape=(
            jax.ShapeDtypeStruct(kernel.shape, f32),
            jax.ShapeDtypeStruct(prod.shape, f32),
        ),
        in_specs=[vmem] * 2,
        out_specs=[pl.BlockSpec(memory_space=pltpu.MemorySpace.HBM)] * 2,
        scratch_shapes=[dma((COPIES + 1,))],
        compiler_params=pltpu.CompilerParams(vmem_limit_bytes=result + 4 * 2**20),
    )(kernel, prod)
    return (kernel, prod.T)


def solution(mesh):
    return jax.shard_map(
        functools.partial(body, mesh.shape["row"], mesh.shape["col"]),
        mesh=mesh,
        in_specs=(
            P(("row", "col"), None),
            P(("row", "col")),
            P(),
            P(("row", "col")),
            P(("row", "col"), None),
        ),
        out_specs=(P("row", "col"), P(("row", "col"), None)),
        check_vma=False,
    )
```

time: 61.7 us -> 58 us (0.940)
  other arithmetic: 1.69 us -> 0 us
  Pallas kernels: 58.6 us -> 57 us
  local copies, waits for them, and re-layouts: 0.63 us -> 0 us
    pallas_call x1, Pallas kernels: 58.6 us -> 55.4 us  [body(): pl.pallas_call(functools.partial(exchange_kernel, n_row, n_col, chunks, p...]
    convert_element_type x1 -> x0, other arithmetic: 1.69 us -> none  [body(): return (kernel.astype(f32), prod.T)]
    pallas_call x0 -> x1, Pallas kernels: none -> 1.56 us  [body(): pl.pallas_call(write_kernel, out_shape=(jax.ShapeDtypeStruct(kernel.shape...]
    unnamed x1 -> x0, local copies, waits for them, and re-layouts: 0.63 us -> none
where the time goes in v3:
time: 58 us; the launch traced here: 57.8 us
  Pallas kernels  57 us (98%)
  between operations  0.8 us (1%)
    pallas_call x1, Pallas kernels, body(): pl.pallas_call(functools.partial(exchange_kernel, n_row, n_col, chunks, p...  55.4 us
    pallas_call x1, Pallas kernels, body(): pl.pallas_call(write_kernel, out_shape=(jax.ShapeDtypeStruct(kernel.shape...  1.56 us

profile of v3, /device:TPU:0, one launch (start us, length us, event | category | flops | bytes accessed | tf_op | source)
XLA Modules:
  0.0 57.8 jit_solution(23027183612063821)
XLA Ops:
  0.6 55.4 %shard_map.68 = (f32[576,1152]{1,0:T(8,128)S(1)}, f32[64,144]{1,0:T(8,128)S(1)}) custom-call(bf16[144,3072]{1,0:T(8,128)(2,1)} %raw_hbm.1, s32[1,16]{1,0:T(1,128)} %bitcast.8, f32[1,144]{1,0:T(1,128)} %bitcast.7, bf16[64,144]{1,0:T(8,128)(2,1)} %bitcast.5, f32[1,3072]{1,0:T(1,128)} %bitcast.6), custom_call_target="tpu_custom_call" | custom-call | tf_op jit(solution)/shard_map/pallas_call | solution.py:623
  56.1 1.6 %shard_map.69 = (f32[576,1152]{1,0:T(8,128)}, f32[64,144]{1,0:T(8,128)}) custom-call(f32[576,1152]{1,0:T(8,128)S(1)} %get-tuple-element.6.kernel_ref, f32[64,144]{1,0:T(8,128)S(1)} %get-tuple-element.7.prod_ref), custom_call_target="tpu_custom_call" | custom-call | tf_op jit(solution)/shard_map/pallas_call | solution.py:636
